TPU v7x, 32 devices: a whole 2x2x4 slice. The times are simulated.
32 devices in a mesh: gx: 4 (over y, x), gy: 4 (over z), gz: 2 (over core).
Axes of the slice: x: 2, y: 2, z: 4, core: 2. Of those that a mesh axis runs over, the one named last changes fastest.
Arguments:
- load: float32 [256, 256, 256], P('gx', 'gy', 'gz'), may hold values from -12 to 12
- stiffness: float32 [256, 256, 256], P('gx', 'gy', 'gz'), may hold values from 0.02 to 2
- prestress: float32 [256, 256], P(('gx', 'gy'), 'gz'), may hold values from -3 to 3
- state_var: float32 [256, 256], P(('gx', 'gy'), 'gz'), may hold values from -1 to 1
- normal_a: float32 [256, 256], P(('gx', 'gy'), 'gz'), may hold values from 1 to 3
Outputs:
- displacement: float32 [256, 256, 256], P('gx', 'gy', 'gz')
- slip_rate: float32 [256, 256], P(('gx', 'gy'), 'gz')
All inputs are finite; a program needn't handle non-finite values.
Results may differ from a plain program's by a relative error of at most 0.0003.
Values sent between devices are 32-bit elements; how exact they have to be, the bound alone decides.
A program may use at most 128 MiB of HBM per device.

v0:
```python
import jax
import jax.numpy as jnp
from jax import lax
from jax.sharding import PartitionSpec as P

ITERS = 3


def extended(cells, sides, width):
    for axis, dim in sides:
        count = lax.axis_size(axis)
        ends = count - 1
        head = lax.slice_in_dim(cells, 0, width, axis=dim)
        tail = lax.slice_in_dim(cells, cells.shape[dim] - width, cells.shape[dim], axis=dim)
        cells = jnp.concatenate(
            [
                lax.ppermute(tail, axis, [(i, (i + 1) % count) for i in range(ends)]),
                cells,
                lax.ppermute(head, axis, [((i + 1) % count, i) for i in range(ends)]),
            ],
            axis=dim,
        )
    return cells


def shifted(padded, sizes_now, axis_num, offset):
    slicers = [slice(2, 2 + sizes_now[0]), slice(2, 2 + sizes_now[1]), slice(2, 2 + sizes_now[2])]
    slicers[axis_num] = slice(2 + offset, 2 + offset + sizes_now[axis_num])
    return padded[tuple(slicers)]


def operate(field, stiffness):
    padded = extended(field, (("gx", 0), ("gy", 1), ("gz", 2)), 2)
    sizes_now = field.shape
    near_sum = jnp.zeros_like(field)
    for axis_num in range(3):
        near_sum = near_sum + 16.0 * (
            shifted(padded, sizes_now, axis_num, 1) + shifted(padded, sizes_now, axis_num, -1)
        )
        near_sum = near_sum - (
            shifted(padded, sizes_now, axis_num, 2) + shifted(padded, sizes_now, axis_num, -2)
        )
    return (7.5 + stiffness) * field - near_sum / 12.0


def paired_sums(residual, precond, image):
    return lax.psum((jnp.sum(residual * precond), jnp.sum(image * precond)), ("gx", "gy", "gz"))


def per_device(load, stiffness, prestress, state_var, normal_a):
    inverse = 1.0 / (7.5 + stiffness)
    solution = jnp.zeros_like(load)
    residual = load
    precond = inverse * residual
    image = operate(precond, stiffness)
    gamma, delta = paired_sums(residual, precond, image)
    alpha = gamma / delta
    direction = precond
    along = image
    for iteration in range(ITERS):
        solution = solution + alpha * direction
        residual = residual - alpha * along
        if iteration + 1 < ITERS:
            precond = inverse * residual
            image = operate(precond, stiffness)
            gamma_new, delta = paired_sums(residual, precond, image)
            ratio = gamma_new / gamma
            alpha = gamma_new / (delta - ratio * gamma_new / alpha)
            direction = precond + ratio * direction
            along = image + ratio * along
            gamma = gamma_new
    rows_y = solution.shape[1]
    total_y = rows_y * lax.axis_size("gy")
    edge_rows = jnp.concatenate((solution[:, :2, :], solution[:, rows_y - 2 :, :]), axis=1)
    local_rows = jnp.array([0, 1, rows_y - 2, rows_y - 1], dtype=jnp.int32)
    global_y = lax.axis_index("gy") * rows_y + local_rows
    offset = global_y - (total_y // 2 - 2)
    weights = (
        (offset == 0).astype(jnp.float32)
        - 27.0 * (offset == 1).astype(jnp.float32)
        + 27.0 * (offset == 2).astype(jnp.float32)
        - (offset == 3).astype(jnp.float32)
    ) / 24.0
    fault_term = jnp.sum(edge_rows * weights[None, :, None], axis=1)
    owned_rows = solution.shape[0] // lax.axis_size("gy")
    whole_strip = lax.psum(fault_term, "gy")
    traction = lax.dynamic_slice_in_dim(
        whole_strip, lax.axis_index("gy") * owned_rows, owned_rows, 0
    )
    slip_rate = jnp.exp(-state_var) * jnp.sinh((prestress + 2.0 * traction) / normal_a)
    return (solution, slip_rate)


def solution(mesh):
    placed = (
        P("gx", "gy", "gz"),
        P("gx", "gy", "gz"),
        P(("gx", "gy"), "gz"),
        P(("gx", "gy"), "gz"),
        P(("gx", "gy"), "gz"),
    )
    return jax.shard_map(
        per_device,
        mesh=mesh,
        in_specs=placed,
        out_specs=(P("gx", "gy", "gz"), P(("gx", "gy"), "gz")),
        check_vma=False,
    )
```

profile of v0, /device:TPU:0, one launch (start us, length us, event | category | flops | bytes accessed | tf_op | source)
XLA Modules:
  0.0 352.4 jit_solution(6903636222099214039)
XLA Ops:
  0.6 4.7 %copy_multiply_fusion = f32[64,64,128]{2,0,1:T(8,128)S(1)} fusion(f32[64,64,128]{2,1,0:T(8,128)} %param.6, f32[64,64,128]{2,1,0:T(8,128)} %param.7), kind=kLoop, calls=%fused_computation.122 | loop fusion | flops 1572864 | bytes 6291456 | tf_op jit(solution)/shard_map/mul | solution.py:54
  5.3 1.3 collective-permute-start
  6.6 5.5 %collective-permute-start.1 = (f32[2,64,128]{2,0,1:T(2,128)S(1)}, f32[2,64,128]{2,0,1:T(2,128)S(1)}, u32[]{:S(2)}, u32[]{:S(2)}) collective-permute-start(f32[2,64,128]{2,0,1:T(2,128)S(1)} %get-tuple-element.48), channel_id=1, source_target_pairs={{0,8},{8,16},{16,24},{1,9},{9,17},{17,25},{2,10},{10,18},{18,26},{... | collective-permute-start | bytes 196616 | tf_op jit(solution)/shard_map/ppermute | solution.py:17
  12.5 1.6 collective-permute-done.1
  15.4 4.6 %collective-permute-start.3 = (f32[68,2,128]{2,0,1:T(8,128)S(1)}, f32[68,2,128]{2,0,1:T(8,128)S(1)}, u32[]{:S(2)}, u32[]{:S(2)}) collective-permute-start(f32[68,2,128]{2,0,1:T(8,128)S(1)} %get-tuple-element.40), channel_id=1, source_target_pairs={{0,2},{2,4},{4,6},{1,3},{3,5},{5,7},{8,10},{10,12},{12,14},{9,11},... | collective-permute-start | bytes 208904 | tf_op jit(solution)/shard_map/ppermute | solution.py:17
  20.4 1.6 collective-permute-done.3
  22.3 3.0 fusion.63
  25.3 2.6 copy.112
  27.9 1.3 collective-permute-start.5
  29.2 2.6 copy.110
  33.1 2.6 pad_maximum_fusion.3
  35.8 2.4 copy.113
  38.2 2.4 copy.111
  40.6 13.9 %multiply_reduce_fusion.3 = (f32[]{:T(128)}, f32[]{:T(128)}, f32[64,64,128]{2,0,1:T(8,128)}) fusion(f32[64,64,128]{2,0,1:T(8,128)S(1)} %copy_multiply_fusion, f32[64,64,128]{2,1,0:T(8,128)} %param.6, f32[68,2,128]{2,0,1:T(8,128)S(1)} %collective-permute-done.2, f32[2,64,128]{2,0,1:T(2,128)S(1)} %collective-permute-done, ...), kind=kLoop, calls=%fused_computation.119 | loop fusion | flops 24117248 | bytes 17121544 | tf_op jit(solution)/shard_map/reduce_sum | solution.py:47
  54.5 44.4 %all-reduce.2 = (f32[]{:T(128)}, f32[]{:T(128)}) all-reduce(f32[]{:T(128)} %get-tuple-element.13, f32[]{:T(128)} %get-tuple-element.12), channel_id=1, replica_groups=mesh['gx'=4,'gy'=4,'gz'=2] {'gx','gy','gz'}, use_global_device_ids=true, to_apply=%region_1.0 | all-reduce | flops 2 | bytes 16 | tf_op jit(solution)/shard_map/psum | solution.py:47
  100.3 5.3 %fusion.48 = f32[64,64,128]{2,0,1:T(8,128)S(1)} fusion(f32[64,64,128]{2,0,1:T(8,128)} %get-tuple-element.23, f32[]{:T(128)S(6)} %div.45, f32[64,64,128]{2,1,0:T(8,128)} %param.6, f32[64,64,128]{2,1,0:T(8,128)} %param.7), kind=kLoop, calls=%fused_computation.124 | loop fusion | flops 2621440 | bytes 8388612 | tf_op jit(solution)/shard_map/mul | solution.py:64
  107.0 4.8 %collective-permute-start.7 = (f32[2,64,128]{2,0,1:T(2,128)S(1)}, f32[2,64,128]{2,0,1:T(2,128)S(1)}, u32[]{:S(2)}, u32[]{:S(2)}) collective-permute-start(f32[2,64,128]{2,0,1:T(2,128)S(1)} %get-tuple-element.46), channel_id=1, source_target_pairs={{0,8},{8,16},{16,24},{1,9},{9,17},{17,25},{2,10},{10,18},{18,26},{... | collective-permute-start | bytes 196616 | tf_op jit(solution)/shard_map/ppermute | solution.py:17
  112.1 1.6 collective-permute-done.7
  115.0 4.5 %collective-permute-start.9 = (f32[68,2,128]{2,0,1:T(8,128)S(1)}, f32[68,2,128]{2,0,1:T(8,128)S(1)}, u32[]{:S(2)}, u32[]{:S(2)}) collective-permute-start(f32[68,2,128]{2,0,1:T(8,128)S(1)} %get-tuple-element.36), channel_id=1, source_target_pairs={{0,2},{2,4},{4,6},{1,3},{3,5},{5,7},{8,10},{10,12},{12,14},{9,11},... | collective-permute-start | bytes 208904 | tf_op jit(solution)/shard_map/ppermute | solution.py:17
  120.0 1.6 collective-permute-done.9
  121.9 3.0 fusion.62
  124.9 2.6 copy.117
  127.5 1.3 collective-permute-start.11
  128.8 2.6 copy.115
  132.7 5.0 %pad_maximum_fusion.4 = (f32[68,66,128]{2,0,1:T(8,128)}, f32[68,66,128]{2,0,1:T(8,128)}) fusion(f32[68,2,128]{2,0,1:T(8,128)S(1)} %collective-permute-done.8, f32[2,64,128]{2,0,1:T(2,128)S(1)} %collective-permute-done.6, f32[64,64,128]{2,0,1:T(8,128)} %copy-done.1, f32[2,64,128]{2,0,1:T(2,128)S(1)} %collective-permute-done.7, ...), kind=kLoop, calls=%fused_computation.5 | loop fusion | flops 3446784 | bytes 6963200 | tf_op jit(solution)/shard_map/concatenate | solution.py:15
  137.7 2.4 copy.118
  140.1 2.4 copy.116
  142.5 22.0 %multiply_reduce_fusion.1 = (f32[]{:T(128)}, f32[]{:T(128)}, f32[64,64,128]{2,0,1:T(8,128)}) fusion(f32[64,64,128]{2,0,1:T(8,128)} %copy-done.1, f32[64,64,128]{2,0,1:T(8,128)} %get-tuple-element.23, f32[]{:T(128)S(6)} %div.45, f32[64,64,128]{2,1,0:T(8,128)} %param.6, f32[68,2,128]{2,0,1:T(8,128)S(1)} %collective-permute-done.8, ...), kind=kLoop, calls=%fused_computation.116 | loop fusion | flops 25165824 | bytes 19218700 | tf_op jit(solution)/shard_map/reduce_sum | solution.py:47
  164.5 44.4 %all-reduce.1 = (f32[]{:T(128)}, f32[]{:T(128)}) all-reduce(f32[]{:T(128)} %get-tuple-element.11, f32[]{:T(128)} %get-tuple-element.10), channel_id=1, replica_groups=mesh['gx'=4,'gy'=4,'gz'=2] {'gx','gy','gz'}, use_global_device_ids=true, to_apply=%region_5.0 | all-reduce | flops 2 | bytes 16 | tf_op jit(solution)/shard_map/psum | solution.py:47
  213.5 6.6 %multiply_reduce_fusion = (f32[]{:T(128)}, f32[64,64,128]{2,0,1:T(8,128)S(1)}) fusion(f32[64,64,128]{2,1,0:T(8,128)} %param.7, f32[64,64,128]{2,0,1:T(8,128)} %get-tuple-element.22, f32[64,64,128]{2,0,1:T(8,128)} %get-tuple-element.23, f32[]{:T(128)S(6)} %div.47, f32[]{:T(128)S(6)} %div.49, f32[]{:T(128)S(6)} %div.45, f32[64,64,128]{2,1,0:T(8,128)} %param.6), kind=kLoop, calls=%fused_computation.114 | loop fusion | flops 5767167 | bytes 10485776 | tf_op jit(solution)/shard_map/reduce_sum | solution.py:47
  220.1 1.3 copy-done
  222.8 4.8 %collective-permute-start.13 = (f32[2,64,128]{2,0,1:T(2,128)S(1)}, f32[2,64,128]{2,0,1:T(2,128)S(1)}, u32[]{:S(2)}, u32[]{:S(2)}) collective-permute-start(f32[2,64,128]{2,0,1:T(2,128)S(1)} %get-tuple-element.44), channel_id=1, source_target_pairs={{0,8},{8,16},{16,24},{1,9},{9,17},{17,25},{2,10},{10,18},{18,26},{... | collective-permute-start | bytes 196616 | tf_op jit(solution)/shard_map/ppermute | solution.py:17
  227.9 1.6 collective-permute-done.13
  231.7 4.5 %collective-permute-start.15 = (f32[68,2,128]{2,0,1:T(8,128)S(1)}, f32[68,2,128]{2,0,1:T(8,128)S(1)}, u32[]{:S(2)}, u32[]{:S(2)}) collective-permute-start(f32[68,2,128]{2,0,1:T(8,128)S(1)} %get-tuple-element.32), channel_id=1, source_target_pairs={{0,2},{2,4},{4,6},{1,3},{3,5},{5,7},{8,10},{10,12},{12,14},{9,11},... | collective-permute-start | bytes 208904 | tf_op jit(solution)/shard_map/ppermute | solution.py:17
  236.7 1.6 collective-permute-done.15
  238.2 1.8 pad_maximum_fusion.2
  240.1 3.0 fusion.61
  243.1 2.6 copy.121
  245.7 1.3 collective-permute-start.17
  247.0 2.6 copy.119
  250.9 5.0 %pad_maximum_fusion.5 = (f32[68,66,128]{2,0,1:T(8,128)}, f32[68,66,128]{2,0,1:T(8,128)}) fusion(f32[68,2,128]{2,0,1:T(8,128)S(1)} %collective-permute-done.14, f32[2,64,128]{2,0,1:T(2,128)S(1)} %collective-permute-done.12, f32[64,64,128]{2,0,1:T(8,128)} %copy-done, f32[2,64,128]{2,0,1:T(2,128)S(1)} %collective-permute-done.13, ...), kind=kLoop, calls=%fused_computation.7 | loop fusion | flops 3446784 | bytes 6963200 | tf_op jit(solution)/shard_map/concatenate | solution.py:15
  255.9 2.4 copy.122
  258.3 2.4 copy.120
  260.7 19.1 %fusion.46 = f32[]{:T(128)} fusion(f32[64,64,128]{2,0,1:T(8,128)} %copy-done, f32[68,2,128]{2,0,1:T(8,128)S(1)} %collective-permute-done.14, f32[2,64,128]{2,0,1:T(2,128)S(1)} %collective-permute-done.12, f32[2,64,128]{2,0,1:T(2,128)S(1)} %collective-permute-done.13, f32[68,2,128]{2,0,1:T(8,128)S(1)} %collective-permute-done.15, f32[68,68,2]{2,0,1:T(8,128)} %copy.122, ...), kind=kLoop, calls=%fused_computation.121 | loop fusion | flops 23068672 | bytes 12927236 | tf_op jit(solution)/shard_map/reduce_sum | solution.py:47
  279.8 44.4 %all-reduce = (f32[]{:T(128)}, f32[]{:T(128)}) all-reduce(f32[]{:T(128)} %get-tuple-element.20, f32[]{:T(128)} %fusion.46), channel_id=1, replica_groups=mesh['gx'=4,'gy'=4,'gz'=2] {'gx','gy','gz'}, use_global_device_ids=true, to_apply=%region_9.0 | all-reduce | flops 2 | bytes 16 | tf_op jit(solution)/shard_map/psum | solution.py:47
  328.1 3.0 multiply_add_fusion
  331.1 2.5 copy.125
  333.8 17.9 %psum.55 = f32[64,128]{1,0:T(8,128)S(1)} all-reduce(f32[64,128]{1,0:T(8,128)S(1)} %fusion.49), channel_id=1, replica_groups=mesh['gx'=4,'gy'=4,'gz'=2] {'gy'}, use_global_device_ids=true, to_apply=%region_13.0 | all-reduce | flops 8192 | bytes 65536 | tf_op jit(solution)/shard_map/psum | solution.py:86
  (43 shorter events, 14.9 us)
Async XLA Ops:
  5.3 7.1 %collective-permute-start = (f32[2,64,128]{2,0,1:T(2,128)S(1)}, f32[2,64,128]{2,0,1:T(2,128)S(1)}, u32[]{:S(2)}, u32[]{:S(2)}) collective-permute-start(f32[2,64,128]{2,0,1:T(2,128)S(1)} %get-tuple-element.49), channel_id=1, source_target_pairs={{8,0},{16,8},{24,16},{9,1},{17,9},{25,17},{10,2},{18,10},{26,18},{... | collective-permute-start | bytes 196616 | tf_op jit(solution)/shard_map/ppermute | solution.py:19
  6.6 7.4 %collective-permute-start.1 = (f32[2,64,128]{2,0,1:T(2,128)S(1)}, f32[2,64,128]{2,0,1:T(2,128)S(1)}, u32[]{:S(2)}, u32[]{:S(2)}) collective-permute-start(f32[2,64,128]{2,0,1:T(2,128)S(1)} %get-tuple-element.48), channel_id=1, source_target_pairs={{0,8},{8,16},{16,24},{1,9},{9,17},{17,25},{2,10},{10,18},{18,26},{... | collective-permute-start | bytes 196616 | tf_op jit(solution)/shard_map/ppermute | solution.py:17
  14.1 6.3 %collective-permute-start.2 = (f32[68,2,128]{2,0,1:T(8,128)S(1)}, f32[68,2,128]{2,0,1:T(8,128)S(1)}, u32[]{:S(2)}, u32[]{:S(2)}) collective-permute-start(f32[68,2,128]{2,0,1:T(8,128)S(1)} %get-tuple-element.41), channel_id=1, source_target_pairs={{2,0},{4,2},{6,4},{3,1},{5,3},{7,5},{10,8},{12,10},{14,12},{11,9},... | collective-permute-start | bytes 208904 | tf_op jit(solution)/shard_map/ppermute | solution.py:19
  15.4 6.6 %collective-permute-start.3 = (f32[68,2,128]{2,0,1:T(8,128)S(1)}, f32[68,2,128]{2,0,1:T(8,128)S(1)}, u32[]{:S(2)}, u32[]{:S(2)}) collective-permute-start(f32[68,2,128]{2,0,1:T(8,128)S(1)} %get-tuple-element.40), channel_id=1, source_target_pairs={{0,2},{2,4},{4,6},{1,3},{3,5},{5,7},{8,10},{10,12},{12,14},{9,11},... | collective-permute-start | bytes 208904 | tf_op jit(solution)/shard_map/ppermute | solution.py:17
  27.9 7.8 %collective-permute-start.5 = (f32[68,68,2]{1,0,2:T(8,128)S(1)}, f32[68,68,2]{1,0,2:T(8,128)S(1)}, u32[]{:S(2)}, u32[]{:S(2)}) collective-permute-start(f32[68,68,2]{1,0,2:T(8,128)S(1)} %copy.112), channel_id=1, source_target_pairs={{0,1},{2,3},{4,5},{6,7},{8,9},{10,11},{12,13},{14,15},{16,17},{18,... | collective-permute-start | bytes 110984 | tf_op jit(solution)/shard_map/ppermute | solution.py:17
  31.8 6.3 %collective-permute-start.4 = (f32[68,68,2]{1,0,2:T(8,128)S(1)}, f32[68,68,2]{1,0,2:T(8,128)S(1)}, u32[]{:S(2)}, u32[]{:S(2)}) collective-permute-start(f32[68,68,2]{1,0,2:T(8,128)S(1)} %copy.110), channel_id=1, source_target_pairs={{1,0},{3,2},{5,4},{7,6},{9,8},{11,10},{13,12},{15,14},{17,16},{19,... | collective-permute-start | bytes 110984 | tf_op jit(solution)/shard_map/ppermute | solution.py:19
  105.6 15.9 %copy-start.1 = (f32[64,64,128]{2,0,1:T(8,128)}, f32[64,64,128]{2,0,1:T(8,128)S(1)}, u32[]{:S(2)}) copy-start(f32[64,64,128]{2,0,1:T(8,128)S(1)} %fusion.48) | copy-start | bytes 6291460
  105.7 6.4 %collective-permute-start.6 = (f32[2,64,128]{2,0,1:T(2,128)S(1)}, f32[2,64,128]{2,0,1:T(2,128)S(1)}, u32[]{:S(2)}, u32[]{:S(2)}) collective-permute-start(f32[2,64,128]{2,0,1:T(2,128)S(1)} %get-tuple-element.47), channel_id=1, source_target_pairs={{8,0},{16,8},{24,16},{9,1},{17,9},{25,17},{10,2},{18,10},{26,18},{... | collective-permute-start | bytes 196616 | tf_op jit(solution)/shard_map/ppermute | solution.py:19
  107.0 6.7 %collective-permute-start.7 = (f32[2,64,128]{2,0,1:T(2,128)S(1)}, f32[2,64,128]{2,0,1:T(2,128)S(1)}, u32[]{:S(2)}, u32[]{:S(2)}) collective-permute-start(f32[2,64,128]{2,0,1:T(2,128)S(1)} %get-tuple-element.46), channel_id=1, source_target_pairs={{0,8},{8,16},{16,24},{1,9},{9,17},{17,25},{2,10},{10,18},{18,26},{... | collective-permute-start | bytes 196616 | tf_op jit(solution)/shard_map/ppermute | solution.py:17
  113.7 6.2 %collective-permute-start.8 = (f32[68,2,128]{2,0,1:T(8,128)S(1)}, f32[68,2,128]{2,0,1:T(8,128)S(1)}, u32[]{:S(2)}, u32[]{:S(2)}) collective-permute-start(f32[68,2,128]{2,0,1:T(8,128)S(1)} %get-tuple-element.37), channel_id=1, source_target_pairs={{2,0},{4,2},{6,4},{3,1},{5,3},{7,5},{10,8},{12,10},{14,12},{11,9},... | collective-permute-start | bytes 208904 | tf_op jit(solution)/shard_map/ppermute | solution.py:19
  115.0 6.5 %collective-permute-start.9 = (f32[68,2,128]{2,0,1:T(8,128)S(1)}, f32[68,2,128]{2,0,1:T(8,128)S(1)}, u32[]{:S(2)}, u32[]{:S(2)}) collective-permute-start(f32[68,2,128]{2,0,1:T(8,128)S(1)} %get-tuple-element.36), channel_id=1, source_target_pairs={{0,2},{2,4},{4,6},{1,3},{3,5},{5,7},{8,10},{10,12},{12,14},{9,11},... | collective-permute-start | bytes 208904 | tf_op jit(solution)/shard_map/ppermute | solution.py:17
  127.5 10.2 %collective-permute-start.11 = (f32[68,68,2]{1,0,2:T(8,128)S(1)}, f32[68,68,2]{1,0,2:T(8,128)S(1)}, u32[]{:S(2)}, u32[]{:S(2)}) collective-permute-start(f32[68,68,2]{1,0,2:T(8,128)S(1)} %copy.117), channel_id=1, source_target_pairs={{0,1},{2,3},{4,5},{6,7},{8,9},{10,11},{12,13},{14,15},{16,17},{18,... | collective-permute-start | bytes 110984 | tf_op jit(solution)/shard_map/ppermute | solution.py:17
  131.4 8.7 %collective-permute-start.10 = (f32[68,68,2]{1,0,2:T(8,128)S(1)}, f32[68,68,2]{1,0,2:T(8,128)S(1)}, u32[]{:S(2)}, u32[]{:S(2)}) collective-permute-start(f32[68,68,2]{1,0,2:T(8,128)S(1)} %copy.115), channel_id=1, source_target_pairs={{1,0},{3,2},{5,4},{7,6},{9,8},{11,10},{13,12},{15,14},{17,16},{19,... | collective-permute-start | bytes 110984 | tf_op jit(solution)/shard_map/ppermute | solution.py:19
  220.1 1.3 copy-start
  220.1 16.1 %copy-start.5 = (s32[4]{0:T(128)S(1)}, s32[4]{0:T(128)}, u32[]{:S(2)}) copy-start(s32[4]{0:T(128)} %constant.51.clone) | copy-start | bytes 52
  221.5 6.4 %collective-permute-start.12 = (f32[2,64,128]{2,0,1:T(2,128)S(1)}, f32[2,64,128]{2,0,1:T(2,128)S(1)}, u32[]{:S(2)}, u32[]{:S(2)}) collective-permute-start(f32[2,64,128]{2,0,1:T(2,128)S(1)} %get-tuple-element.45), channel_id=1, source_target_pairs={{8,0},{16,8},{24,16},{9,1},{17,9},{25,17},{10,2},{18,10},{26,18},{... | collective-permute-start | bytes 196616 | tf_op jit(solution)/shard_map/ppermute | solution.py:19
  222.8 6.7 %collective-permute-start.13 = (f32[2,64,128]{2,0,1:T(2,128)S(1)}, f32[2,64,128]{2,0,1:T(2,128)S(1)}, u32[]{:S(2)}, u32[]{:S(2)}) collective-permute-start(f32[2,64,128]{2,0,1:T(2,128)S(1)} %get-tuple-element.44), channel_id=1, source_target_pairs={{0,8},{8,16},{16,24},{1,9},{9,17},{17,25},{2,10},{10,18},{18,26},{... | collective-permute-start | bytes 196616 | tf_op jit(solution)/shard_map/ppermute | solution.py:17
  230.4 6.2 %collective-permute-start.14 = (f32[68,2,128]{2,0,1:T(8,128)S(1)}, f32[68,2,128]{2,0,1:T(8,128)S(1)}, u32[]{:S(2)}, u32[]{:S(2)}) collective-permute-start(f32[68,2,128]{2,0,1:T(8,128)S(1)} %get-tuple-element.33), channel_id=1, source_target_pairs={{2,0},{4,2},{6,4},{3,1},{5,3},{7,5},{10,8},{12,10},{14,12},{11,9},... | collective-permute-start | bytes 208904 | tf_op jit(solution)/shard_map/ppermute | solution.py:19
  231.7 6.5 %collective-permute-start.15 = (f32[68,2,128]{2,0,1:T(8,128)S(1)}, f32[68,2,128]{2,0,1:T(8,128)S(1)}, u32[]{:S(2)}, u32[]{:S(2)}) collective-permute-start(f32[68,2,128]{2,0,1:T(8,128)S(1)} %get-tuple-element.32), channel_id=1, source_target_pairs={{0,2},{2,4},{4,6},{1,3},{3,5},{5,7},{8,10},{10,12},{12,14},{9,11},... | collective-permute-start | bytes 208904 | tf_op jit(solution)/shard_map/ppermute | solution.py:17
  245.7 10.2 %collective-permute-start.17 = (f32[68,68,2]{1,0,2:T(8,128)S(1)}, f32[68,68,2]{1,0,2:T(8,128)S(1)}, u32[]{:S(2)}, u32[]{:S(2)}) collective-permute-start(f32[68,68,2]{1,0,2:T(8,128)S(1)} %copy.121), channel_id=1, source_target_pairs={{0,1},{2,3},{4,5},{6,7},{8,9},{10,11},{12,13},{14,15},{16,17},{18,... | collective-permute-start | bytes 110984 | tf_op jit(solution)/shard_map/ppermute | solution.py:17
  249.6 8.7 %collective-permute-start.16 = (f32[68,68,2]{1,0,2:T(8,128)S(1)}, f32[68,68,2]{1,0,2:T(8,128)S(1)}, u32[]{:S(2)}, u32[]{:S(2)}) collective-permute-start(f32[68,68,2]{1,0,2:T(8,128)S(1)} %copy.119), channel_id=1, source_target_pairs={{1,0},{3,2},{5,4},{7,6},{9,8},{11,10},{13,12},{15,14},{17,16},{19,... | collective-permute-start | bytes 110984 | tf_op jit(solution)/shard_map/ppermute | solution.py:19
  331.1 20.6 %copy-start.2 = (f32[16,128]{1,0:T(8,128)S(1)}, f32[16,128]{1,0:T(8,128)}, u32[]{:S(2)}) copy-start(f32[16,128]{1,0:T(8,128)} %param.10) | copy-start | bytes 24580
  331.1 20.6 %copy-start.3 = (f32[16,128]{1,0:T(8,128)S(1)}, f32[16,128]{1,0:T(8,128)}, u32[]{:S(2)}) copy-start(f32[16,128]{1,0:T(8,128)} %param.8) | copy-start | bytes 24580
  331.1 20.6 %copy-start.4 = (f32[16,128]{1,0:T(8,128)S(1)}, f32[16,128]{1,0:T(8,128)}, u32[]{:S(2)}) copy-start(f32[16,128]{1,0:T(8,128)} %param.9) | copy-start | bytes 24580
where the time goes:
time: 354 us; the launch traced here: 352 us
  blocking collectives  151 us (43%)
  other arithmetic  91.3 us (26%)
  starting transfers between devices  44.4 us (13%)
  local copies, waits for them, and re-layouts  43.1 us (12%)
  waiting for transfers between devices  11.5 us (3%)
  between operations  10.9 us (3%)
    psum x3, blocking collectives, paired_sums(): lax.psum((jnp.sum(residual * precond), jnp.sum(image * precond)), ('gx',...  133 us
    reduce_sum x3, other arithmetic, paired_sums(): jnp.sum(image * precond)  55 us
    ppermute x9, starting transfers between devices, extended(): lax.ppermute(tail, axis, [(i, (i + 1) % count) for i in range(ends)])  32.7 us
    psum x1, blocking collectives, per_device(): whole_strip = lax.psum(fault_term, 'gy')  17.9 us
    slice x6, local copies, waits for them, and re-layouts, extended(): head = lax.slice_in_dim(cells, 0, width, axis=dim)  16.8 us
    concatenate x9, other arithmetic, extended(): jnp.concatenate([lax.ppermute(tail, axis, [(i, (i + 1) % count) for i in...  16 us
    ppermute x9, starting transfers between devices, extended(): lax.ppermute(head, axis, [((i + 1) % count, i) for i in range(ends)])  11.6 us
    mul x2, other arithmetic, per_device(): precond = inverse * residual  9.98 us
  transfers between devices with their start and end apart: 18, of which 12 were waited for; matrix products, arithmetic and copies ran while one was open for 8% of the time, Pallas kernels for 0%

commit v1 on v0

--- a/solution.py
+++ b/solution.py
@@ -4,6 +4,11 @@
 from jax.sharding import PartitionSpec as P
 
 ITERS = 3
+
+
+def by_each_axis(array, one, other):
+    inner = lax.psum(array, one)
+    return lax.psum(inner, other)
 
 
 def extended(cells, sides, width):
@@ -44,7 +49,7 @@
 
 
 def paired_sums(residual, precond, image):
-    return lax.psum((jnp.sum(residual * precond), jnp.sum(image * precond)), ("gx", "gy", "gz"))
+    return by_each_axis((jnp.sum(residual * precond), jnp.sum(image * precond)), ("gy", "gz"), "gx")
 
 
 def per_device(load, stiffness, prestress, state_var, normal_a):

time: 354 us -> 303 us (0.86)
  blocking collectives: 151 us -> 102 us
    psum x3 -> x6, blocking collectives: 133 us -> 85.9 us  [the longest x3 51.8 us: by_each_axis(): inner = lax.psum(array, one)]
  transfers between devices with their start and end apart: 18 -> 18, of which waited for: 12 -> 12; matrix products, arithmetic and copies ran while one was open for 8% -> 9% of each run, Pallas kernels for 0% -> 0%
where the time goes in v1:
time: 303 us; the launch traced here: 302 us
  blocking collectives  102 us (34%)
  other arithmetic  91.2 us (30%)
  starting transfers between devices  43.8 us (14%)
  local copies, waits for them, and re-layouts  43.1 us (14%)
  waiting for transfers between devices  11.5 us (4%)
  between operations  10.4 us (3%)
    reduce_sum x3, other arithmetic, paired_sums(): jnp.sum(image * precond)  54.8 us
    psum x3, blocking collectives, by_each_axis(): inner = lax.psum(array, one)  51.8 us
    psum x3, blocking collectives, by_each_axis(): return lax.psum(inner, other)  34.1 us
    ppermute x9, starting transfers between devices, extended(): lax.ppermute(tail, axis, [(i, (i + 1) % count) for i in range(ends)])  32.2 us
    slice x6, local copies, waits for them, and re-layouts, extended(): head = lax.slice_in_dim(cells, 0, width, axis=dim)  16.8 us
    concatenate x9, other arithmetic, extended(): jnp.concatenate([lax.ppermute(tail, axis, [(i, (i + 1) % count) for i in...  16 us
    psum x1, blocking collectives, per_device(): whole_strip = lax.psum(fault_term, 'gy')  15.8 us
    ppermute x9, starting transfers between devices, extended(): lax.ppermute(head, axis, [((i + 1) % count, i) for i in range(ends)])  11.6 us
  transfers between devices with their start and end apart: 18, of which 12 were waited for; matrix products, arithmetic and copies ran while one was open for 9% of the time, Pallas kernels for 0%

profile of v1, /device:TPU:0, one launch (start us, length us, event | category | flops | bytes accessed | tf_op | source)
XLA Modules:
  0.0 301.7 jit_solution(16403050823120880474)
XLA Ops:
  0.6 4.7 %copy_multiply_fusion = f32[64,64,128]{2,0,1:T(8,128)S(1)} fusion(f32[64,64,128]{2,1,0:T(8,128)} %param.6, f32[64,64,128]{2,1,0:T(8,128)} %param.7), kind=kLoop, calls=%fused_computation.122 | loop fusion | flops 1572864 | bytes 6291456 | tf_op jit(solution)/shard_map/mul | solution.py:59
  6.6 5.5 %collective-permute-start.1 = (f32[2,64,128]{2,0,1:T(2,128)S(1)}, f32[2,64,128]{2,0,1:T(2,128)S(1)}, u32[]{:S(2)}, u32[]{:S(2)}) collective-permute-start(f32[2,64,128]{2,0,1:T(2,128)S(1)} %get-tuple-element.54), channel_id=1, source_target_pairs={{0,8},{8,16},{16,24},{1,9},{9,17},{17,25},{2,10},{10,18},{18,26},{... | collective-permute-start | bytes 196616 | tf_op jit(solution)/shard_map/ppermute | solution.py:22
  12.5 1.6 collective-permute-done.1
  15.4 4.6 %collective-permute-start.3 = (f32[68,2,128]{2,0,1:T(8,128)S(1)}, f32[68,2,128]{2,0,1:T(8,128)S(1)}, u32[]{:S(2)}, u32[]{:S(2)}) collective-permute-start(f32[68,2,128]{2,0,1:T(8,128)S(1)} %get-tuple-element.46), channel_id=1, source_target_pairs={{0,2},{2,4},{4,6},{1,3},{3,5},{5,7},{8,10},{10,12},{12,14},{9,11},... | collective-permute-start | bytes 208904 | tf_op jit(solution)/shard_map/ppermute | solution.py:22
  20.4 1.6 collective-permute-done.3
  22.3 3.0 fusion.63
  25.3 2.6 copy.112
  27.9 1.3 collective-permute-start.5
  29.2 2.6 copy.110
  33.1 2.6 pad_maximum_fusion.3
  35.8 2.4 copy.113
  38.2 2.4 copy.111
  40.6 13.8 %multiply_reduce_fusion.3 = (f32[]{:T(128)}, f32[]{:T(128)}, f32[64,64,128]{2,0,1:T(8,128)}) fusion(f32[64,64,128]{2,0,1:T(8,128)S(1)} %copy_multiply_fusion, f32[64,64,128]{2,1,0:T(8,128)} %param.6, f32[68,2,128]{2,0,1:T(8,128)S(1)} %collective-permute-done.2, f32[2,64,128]{2,0,1:T(2,128)S(1)} %collective-permute-done, ...), kind=kLoop, calls=%fused_computation.119 | loop fusion | flops 24117248 | bytes 17121544 | tf_op jit(solution)/shard_map/reduce_sum | solution.py:52
  54.4 19.8 %all-reduce.2 = (f32[]{:T(128)}, f32[]{:T(128)}) all-reduce(f32[]{:T(128)} %get-tuple-element.13, f32[]{:T(128)} %get-tuple-element.12), channel_id=1, replica_groups=mesh['gx'=4,'gy'=4,'gz'=2] {'gy','gz'}, use_global_device_ids=true, to_apply=%region_1.0 | all-reduce | flops 2 | bytes 16 | tf_op jit(solution)/shard_map/psum | solution.py:10
  74.2 11.6 %all-reduce.5 = (f32[]{:T(128)}, f32[]{:T(128)}) all-reduce(f32[]{:T(128)} %get-tuple-element.18, f32[]{:T(128)} %get-tuple-element.19), channel_id=1, replica_groups=mesh['gx'=4,'gy'=4,'gz'=2] {'gx'}, use_global_device_ids=true, to_apply=%region_2.0 | all-reduce | flops 2 | bytes 16 | tf_op jit(solution)/shard_map/psum | solution.py:11
  87.2 5.3 %fusion.48 = f32[64,64,128]{2,0,1:T(8,128)S(1)} fusion(f32[64,64,128]{2,0,1:T(8,128)} %get-tuple-element.29, f32[]{:T(128)S(6)} %div.45, f32[64,64,128]{2,1,0:T(8,128)} %param.6, f32[64,64,128]{2,1,0:T(8,128)} %param.7), kind=kLoop, calls=%fused_computation.124 | loop fusion | flops 2621440 | bytes 8388612 | tf_op jit(solution)/shard_map/mul | solution.py:69
  93.9 4.5 %collective-permute-start.7 = (f32[2,64,128]{2,0,1:T(2,128)S(1)}, f32[2,64,128]{2,0,1:T(2,128)S(1)}, u32[]{:S(2)}, u32[]{:S(2)}) collective-permute-start(f32[2,64,128]{2,0,1:T(2,128)S(1)} %get-tuple-element.52), channel_id=1, source_target_pairs={{0,8},{8,16},{16,24},{1,9},{9,17},{17,25},{2,10},{10,18},{18,26},{... | collective-permute-start | bytes 196616 | tf_op jit(solution)/shard_map/ppermute | solution.py:22
  98.7 1.6 collective-permute-done.7
  101.6 4.5 %collective-permute-start.9 = (f32[68,2,128]{2,0,1:T(8,128)S(1)}, f32[68,2,128]{2,0,1:T(8,128)S(1)}, u32[]{:S(2)}, u32[]{:S(2)}) collective-permute-start(f32[68,2,128]{2,0,1:T(8,128)S(1)} %get-tuple-element.42), channel_id=1, source_target_pairs={{0,2},{2,4},{4,6},{1,3},{3,5},{5,7},{8,10},{10,12},{12,14},{9,11},... | collective-permute-start | bytes 208904 | tf_op jit(solution)/shard_map/ppermute | solution.py:22
  106.6 1.6 collective-permute-done.9
  108.5 3.0 fusion.62
  111.5 2.6 copy.117
  114.1 1.3 collective-permute-start.11
  115.4 2.6 copy.115
  119.3 5.0 %pad_maximum_fusion.4 = (f32[68,66,128]{2,0,1:T(8,128)}, f32[68,66,128]{2,0,1:T(8,128)}) fusion(f32[68,2,128]{2,0,1:T(8,128)S(1)} %collective-permute-done.8, f32[2,64,128]{2,0,1:T(2,128)S(1)} %collective-permute-done.6, f32[64,64,128]{2,0,1:T(8,128)} %copy-done.1, f32[2,64,128]{2,0,1:T(2,128)S(1)} %collective-permute-done.7, ...), kind=kLoop, calls=%fused_computation.5 | loop fusion | flops 3446784 | bytes 6963200 | tf_op jit(solution)/shard_map/concatenate | solution.py:20
  124.3 2.4 copy.118
  126.7 2.4 copy.116
  129.1 22.1 %multiply_reduce_fusion.1 = (f32[]{:T(128)}, f32[]{:T(128)}, f32[64,64,128]{2,0,1:T(8,128)}) fusion(f32[64,64,128]{2,0,1:T(8,128)} %copy-done.1, f32[64,64,128]{2,0,1:T(8,128)} %get-tuple-element.29, f32[]{:T(128)S(6)} %div.45, f32[64,64,128]{2,1,0:T(8,128)} %param.6, f32[68,2,128]{2,0,1:T(8,128)S(1)} %collective-permute-done.8, ...), kind=kLoop, calls=%fused_computation.116 | loop fusion | flops 25165824 | bytes 19218700 | tf_op jit(solution)/shard_map/reduce_sum | solution.py:52
  151.2 15.3 %all-reduce.1 = (f32[]{:T(128)}, f32[]{:T(128)}) all-reduce(f32[]{:T(128)} %get-tuple-element.11, f32[]{:T(128)} %get-tuple-element.10), channel_id=1, replica_groups=mesh['gx'=4,'gy'=4,'gz'=2] {'gy','gz'}, use_global_device_ids=true, to_apply=%region_7.0 | all-reduce | flops 2 | bytes 16 | tf_op jit(solution)/shard_map/psum | solution.py:10
  166.5 11.1 %all-reduce.4 = (f32[]{:T(128)}, f32[]{:T(128)}) all-reduce(f32[]{:T(128)} %get-tuple-element.16, f32[]{:T(128)} %get-tuple-element.17), channel_id=1, replica_groups=mesh['gx'=4,'gy'=4,'gz'=2] {'gx'}, use_global_device_ids=true, to_apply=%region_8.0 | all-reduce | flops 2 | bytes 16 | tf_op jit(solution)/shard_map/psum | solution.py:11
  181.9 6.6 %multiply_reduce_fusion = (f32[]{:T(128)}, f32[64,64,128]{2,0,1:T(8,128)S(1)}) fusion(f32[64,64,128]{2,1,0:T(8,128)} %param.7, f32[64,64,128]{2,0,1:T(8,128)} %get-tuple-element.28, f32[64,64,128]{2,0,1:T(8,128)} %get-tuple-element.29, f32[]{:T(128)S(6)} %div.47, f32[]{:T(128)S(6)} %div.49, f32[]{:T(128)S(6)} %div.45, f32[64,64,128]{2,1,0:T(8,128)} %param.6), kind=kLoop, calls=%fused_computation.114 | loop fusion | flops 5767167 | bytes 10485776 | tf_op jit(solution)/shard_map/reduce_sum | solution.py:52
  188.5 1.3 copy-done
  191.2 4.6 %collective-permute-start.13 = (f32[2,64,128]{2,0,1:T(2,128)S(1)}, f32[2,64,128]{2,0,1:T(2,128)S(1)}, u32[]{:S(2)}, u32[]{:S(2)}) collective-permute-start(f32[2,64,128]{2,0,1:T(2,128)S(1)} %get-tuple-element.50), channel_id=1, source_target_pairs={{0,8},{8,16},{16,24},{1,9},{9,17},{17,25},{2,10},{10,18},{18,26},{... | collective-permute-start | bytes 196616 | tf_op jit(solution)/shard_map/ppermute | solution.py:22
  199.8 4.5 %collective-permute-start.15 = (f32[68,2,128]{2,0,1:T(8,128)S(1)}, f32[68,2,128]{2,0,1:T(8,128)S(1)}, u32[]{:S(2)}, u32[]{:S(2)}) collective-permute-start(f32[68,2,128]{2,0,1:T(8,128)S(1)} %get-tuple-element.38), channel_id=1, source_target_pairs={{0,2},{2,4},{4,6},{1,3},{3,5},{5,7},{8,10},{10,12},{12,14},{9,11},... | collective-permute-start | bytes 208904 | tf_op jit(solution)/shard_map/ppermute | solution.py:22
  204.7 1.6 collective-permute-done.15
  206.3 1.8 pad_maximum_fusion.2
  208.2 3.0 fusion.61
  211.2 2.6 copy.121
  215.1 2.6 copy.119
  219.0 5.0 %pad_maximum_fusion.5 = (f32[68,66,128]{2,0,1:T(8,128)}, f32[68,66,128]{2,0,1:T(8,128)}) fusion(f32[68,2,128]{2,0,1:T(8,128)S(1)} %collective-permute-done.14, f32[2,64,128]{2,0,1:T(2,128)S(1)} %collective-permute-done.12, f32[64,64,128]{2,0,1:T(8,128)} %copy-done, f32[2,64,128]{2,0,1:T(2,128)S(1)} %collective-permute-done.13, ...), kind=kLoop, calls=%fused_computation.7 | loop fusion | flops 3446784 | bytes 6963200 | tf_op jit(solution)/shard_map/concatenate | solution.py:20
  223.9 2.4 copy.122
  226.3 2.4 copy.120
  228.7 19.0 %fusion.46 = f32[]{:T(128)} fusion(f32[64,64,128]{2,0,1:T(8,128)} %copy-done, f32[68,2,128]{2,0,1:T(8,128)S(1)} %collective-permute-done.14, f32[2,64,128]{2,0,1:T(2,128)S(1)} %collective-permute-done.12, f32[2,64,128]{2,0,1:T(2,128)S(1)} %collective-permute-done.13, f32[68,2,128]{2,0,1:T(8,128)S(1)} %collective-permute-done.15, f32[68,68,2]{2,0,1:T(8,128)} %copy.122, ...), kind=kLoop, calls=%fused_computation.121 | loop fusion | flops 23068672 | bytes 12927236 | tf_op jit(solution)/shard_map/reduce_sum | solution.py:52
  247.7 16.6 %all-reduce = (f32[]{:T(128)}, f32[]{:T(128)}) all-reduce(f32[]{:T(128)} %get-tuple-element.26, f32[]{:T(128)} %fusion.46), channel_id=1, replica_groups=mesh['gx'=4,'gy'=4,'gz'=2] {'gy','gz'}, use_global_device_ids=true, to_apply=%region_13.0 | all-reduce | flops 2 | bytes 16 | tf_op jit(solution)/shard_map/psum | solution.py:10
  264.4 11.4 %all-reduce.3 = (f32[]{:T(128)}, f32[]{:T(128)}) all-reduce(f32[]{:T(128)} %get-tuple-element.14, f32[]{:T(128)} %get-tuple-element.15), channel_id=1, replica_groups=mesh['gx'=4,'gy'=4,'gz'=2] {'gx'}, use_global_device_ids=true, to_apply=%region_14.0 | all-reduce | flops 2 | bytes 16 | tf_op jit(solution)/shard_map/psum | solution.py:11
  279.6 3.0 multiply_add_fusion
  282.6 2.5 copy.125
  285.3 15.8 %psum.103 = f32[64,128]{1,0:T(8,128)S(1)} all-reduce(f32[64,128]{1,0:T(8,128)S(1)} %fusion.49), channel_id=1, replica_groups=mesh['gx'=4,'gy'=4,'gz'=2] {'gy'}, use_global_device_ids=true, to_apply=%region_19.0 | all-reduce | flops 8192 | bytes 65536 | tf_op jit(solution)/shard_map/psum | solution.py:91
  (46 shorter events, 19.1 us)
Async XLA Ops:
  5.3 7.1 %collective-permute-start = (f32[2,64,128]{2,0,1:T(2,128)S(1)}, f32[2,64,128]{2,0,1:T(2,128)S(1)}, u32[]{:S(2)}, u32[]{:S(2)}) collective-permute-start(f32[2,64,128]{2,0,1:T(2,128)S(1)} %get-tuple-element.55), channel_id=1, source_target_pairs={{8,0},{16,8},{24,16},{9,1},{17,9},{25,17},{10,2},{18,10},{26,18},{... | collective-permute-start | bytes 196616 | tf_op jit(solution)/shard_map/ppermute | solution.py:24
  6.6 7.4 %collective-permute-start.1 = (f32[2,64,128]{2,0,1:T(2,128)S(1)}, f32[2,64,128]{2,0,1:T(2,128)S(1)}, u32[]{:S(2)}, u32[]{:S(2)}) collective-permute-start(f32[2,64,128]{2,0,1:T(2,128)S(1)} %get-tuple-element.54), channel_id=1, source_target_pairs={{0,8},{8,16},{16,24},{1,9},{9,17},{17,25},{2,10},{10,18},{18,26},{... | collective-permute-start | bytes 196616 | tf_op jit(solution)/shard_map/ppermute | solution.py:22
  14.1 6.3 %collective-permute-start.2 = (f32[68,2,128]{2,0,1:T(8,128)S(1)}, f32[68,2,128]{2,0,1:T(8,128)S(1)}, u32[]{:S(2)}, u32[]{:S(2)}) collective-permute-start(f32[68,2,128]{2,0,1:T(8,128)S(1)} %get-tuple-element.47), channel_id=1, source_target_pairs={{2,0},{4,2},{6,4},{3,1},{5,3},{7,5},{10,8},{12,10},{14,12},{11,9},... | collective-permute-start | bytes 208904 | tf_op jit(solution)/shard_map/ppermute | solution.py:24
  15.4 6.6 %collective-permute-start.3 = (f32[68,2,128]{2,0,1:T(8,128)S(1)}, f32[68,2,128]{2,0,1:T(8,128)S(1)}, u32[]{:S(2)}, u32[]{:S(2)}) collective-permute-start(f32[68,2,128]{2,0,1:T(8,128)S(1)} %get-tuple-element.46), channel_id=1, source_target_pairs={{0,2},{2,4},{4,6},{1,3},{3,5},{5,7},{8,10},{10,12},{12,14},{9,11},... | collective-permute-start | bytes 208904 | tf_op jit(solution)/shard_map/ppermute | solution.py:22
  27.9 7.8 %collective-permute-start.5 = (f32[68,68,2]{1,0,2:T(8,128)S(1)}, f32[68,68,2]{1,0,2:T(8,128)S(1)}, u32[]{:S(2)}, u32[]{:S(2)}) collective-permute-start(f32[68,68,2]{1,0,2:T(8,128)S(1)} %copy.112), channel_id=1, source_target_pairs={{0,1},{2,3},{4,5},{6,7},{8,9},{10,11},{12,13},{14,15},{16,17},{18,... | collective-permute-start | bytes 110984 | tf_op jit(solution)/shard_map/ppermute | solution.py:22
  31.8 6.3 %collective-permute-start.4 = (f32[68,68,2]{1,0,2:T(8,128)S(1)}, f32[68,68,2]{1,0,2:T(8,128)S(1)}, u32[]{:S(2)}, u32[]{:S(2)}) collective-permute-start(f32[68,68,2]{1,0,2:T(8,128)S(1)} %copy.110), channel_id=1, source_target_pairs={{1,0},{3,2},{5,4},{7,6},{9,8},{11,10},{13,12},{15,14},{17,16},{19,... | collective-permute-start | bytes 110984 | tf_op jit(solution)/shard_map/ppermute | solution.py:24
  92.5 15.7 %copy-start.1 = (f32[64,64,128]{2,0,1:T(8,128)}, f32[64,64,128]{2,0,1:T(8,128)S(1)}, u32[]{:S(2)}) copy-start(f32[64,64,128]{2,0,1:T(8,128)S(1)} %fusion.48) | copy-start | bytes 6291460
  92.6 6.2 %collective-permute-start.6 = (f32[2,64,128]{2,0,1:T(2,128)S(1)}, f32[2,64,128]{2,0,1:T(2,128)S(1)}, u32[]{:S(2)}, u32[]{:S(2)}) collective-permute-start(f32[2,64,128]{2,0,1:T(2,128)S(1)} %get-tuple-element.53), channel_id=1, source_target_pairs={{8,0},{16,8},{24,16},{9,1},{17,9},{25,17},{10,2},{18,10},{26,18},{... | collective-permute-start | bytes 196616 | tf_op jit(solution)/shard_map/ppermute | solution.py:24
  93.9 6.4 %collective-permute-start.7 = (f32[2,64,128]{2,0,1:T(2,128)S(1)}, f32[2,64,128]{2,0,1:T(2,128)S(1)}, u32[]{:S(2)}, u32[]{:S(2)}) collective-permute-start(f32[2,64,128]{2,0,1:T(2,128)S(1)} %get-tuple-element.52), channel_id=1, source_target_pairs={{0,8},{8,16},{16,24},{1,9},{9,17},{17,25},{2,10},{10,18},{18,26},{... | collective-permute-start | bytes 196616 | tf_op jit(solution)/shard_map/ppermute | solution.py:22
  100.3 6.2 %collective-permute-start.8 = (f32[68,2,128]{2,0,1:T(8,128)S(1)}, f32[68,2,128]{2,0,1:T(8,128)S(1)}, u32[]{:S(2)}, u32[]{:S(2)}) collective-permute-start(f32[68,2,128]{2,0,1:T(8,128)S(1)} %get-tuple-element.43), channel_id=1, source_target_pairs={{2,0},{4,2},{6,4},{3,1},{5,3},{7,5},{10,8},{12,10},{14,12},{11,9},... | collective-permute-start | bytes 208904 | tf_op jit(solution)/shard_map/ppermute | solution.py:24
  101.6 6.5 %collective-permute-start.9 = (f32[68,2,128]{2,0,1:T(8,128)S(1)}, f32[68,2,128]{2,0,1:T(8,128)S(1)}, u32[]{:S(2)}, u32[]{:S(2)}) collective-permute-start(f32[68,2,128]{2,0,1:T(8,128)S(1)} %get-tuple-element.42), channel_id=1, source_target_pairs={{0,2},{2,4},{4,6},{1,3},{3,5},{5,7},{8,10},{10,12},{12,14},{9,11},... | collective-permute-start | bytes 208904 | tf_op jit(solution)/shard_map/ppermute | solution.py:22
  114.1 10.2 %collective-permute-start.11 = (f32[68,68,2]{1,0,2:T(8,128)S(1)}, f32[68,68,2]{1,0,2:T(8,128)S(1)}, u32[]{:S(2)}, u32[]{:S(2)}) collective-permute-start(f32[68,68,2]{1,0,2:T(8,128)S(1)} %copy.117), channel_id=1, source_target_pairs={{0,1},{2,3},{4,5},{6,7},{8,9},{10,11},{12,13},{14,15},{16,17},{18,... | collective-permute-start | bytes 110984 | tf_op jit(solution)/shard_map/ppermute | solution.py:22
  118.0 8.7 %collective-permute-start.10 = (f32[68,68,2]{1,0,2:T(8,128)S(1)}, f32[68,68,2]{1,0,2:T(8,128)S(1)}, u32[]{:S(2)}, u32[]{:S(2)}) collective-permute-start(f32[68,68,2]{1,0,2:T(8,128)S(1)} %copy.115), channel_id=1, source_target_pairs={{1,0},{3,2},{5,4},{7,6},{9,8},{11,10},{13,12},{15,14},{17,16},{19,... | collective-permute-start | bytes 110984 | tf_op jit(solution)/shard_map/ppermute | solution.py:24
  188.5 1.3 copy-start
  188.5 15.9 %copy-start.5 = (s32[4]{0:T(128)S(1)}, s32[4]{0:T(128)}, u32[]{:S(2)}) copy-start(s32[4]{0:T(128)} %constant.51.clone) | copy-start | bytes 52
  189.9 6.6 %collective-permute-start.12 = (f32[2,64,128]{2,0,1:T(2,128)S(1)}, f32[2,64,128]{2,0,1:T(2,128)S(1)}, u32[]{:S(2)}, u32[]{:S(2)}) collective-permute-start(f32[2,64,128]{2,0,1:T(2,128)S(1)} %get-tuple-element.51), channel_id=1, source_target_pairs={{8,0},{16,8},{24,16},{9,1},{17,9},{25,17},{10,2},{18,10},{26,18},{... | collective-permute-start | bytes 196616 | tf_op jit(solution)/shard_map/ppermute | solution.py:24
  191.2 6.4 %collective-permute-start.13 = (f32[2,64,128]{2,0,1:T(2,128)S(1)}, f32[2,64,128]{2,0,1:T(2,128)S(1)}, u32[]{:S(2)}, u32[]{:S(2)}) collective-permute-start(f32[2,64,128]{2,0,1:T(2,128)S(1)} %get-tuple-element.50), channel_id=1, source_target_pairs={{0,8},{8,16},{16,24},{1,9},{9,17},{17,25},{2,10},{10,18},{18,26},{... | collective-permute-start | bytes 196616 | tf_op jit(solution)/shard_map/ppermute | solution.py:22
  198.5 6.2 %collective-permute-start.14 = (f32[68,2,128]{2,0,1:T(8,128)S(1)}, f32[68,2,128]{2,0,1:T(8,128)S(1)}, u32[]{:S(2)}, u32[]{:S(2)}) collective-permute-start(f32[68,2,128]{2,0,1:T(8,128)S(1)} %get-tuple-element.39), channel_id=1, source_target_pairs={{2,0},{4,2},{6,4},{3,1},{5,3},{7,5},{10,8},{12,10},{14,12},{11,9},... | collective-permute-start | bytes 208904 | tf_op jit(solution)/shard_map/ppermute | solution.py:24
  199.8 6.5 %collective-permute-start.15 = (f32[68,2,128]{2,0,1:T(8,128)S(1)}, f32[68,2,128]{2,0,1:T(8,128)S(1)}, u32[]{:S(2)}, u32[]{:S(2)}) collective-permute-start(f32[68,2,128]{2,0,1:T(8,128)S(1)} %get-tuple-element.38), channel_id=1, source_target_pairs={{0,2},{2,4},{4,6},{1,3},{3,5},{5,7},{8,10},{10,12},{12,14},{9,11},... | collective-permute-start | bytes 208904 | tf_op jit(solution)/shard_map/ppermute | solution.py:22
  213.8 10.2 %collective-permute-start.17 = (f32[68,68,2]{1,0,2:T(8,128)S(1)}, f32[68,68,2]{1,0,2:T(8,128)S(1)}, u32[]{:S(2)}, u32[]{:S(2)}) collective-permute-start(f32[68,68,2]{1,0,2:T(8,128)S(1)} %copy.121), channel_id=1, source_target_pairs={{0,1},{2,3},{4,5},{6,7},{8,9},{10,11},{12,13},{14,15},{16,17},{18,... | collective-permute-start | bytes 110984 | tf_op jit(solution)/shard_map/ppermute | solution.py:22
  217.7 8.7 %collective-permute-start.16 = (f32[68,68,2]{1,0,2:T(8,128)S(1)}, f32[68,68,2]{1,0,2:T(8,128)S(1)}, u32[]{:S(2)}, u32[]{:S(2)}) collective-permute-start(f32[68,68,2]{1,0,2:T(8,128)S(1)} %copy.119), channel_id=1, source_target_pairs={{1,0},{3,2},{5,4},{7,6},{9,8},{11,10},{13,12},{15,14},{17,16},{19,... | collective-permute-start | bytes 110984 | tf_op jit(solution)/shard_map/ppermute | solution.py:24
  282.6 18.4 %copy-start.2 = (f32[16,128]{1,0:T(8,128)S(1)}, f32[16,128]{1,0:T(8,128)}, u32[]{:S(2)}) copy-start(f32[16,128]{1,0:T(8,128)} %param.10) | copy-start | bytes 24580
  282.6 18.4 %copy-start.3 = (f32[16,128]{1,0:T(8,128)S(1)}, f32[16,128]{1,0:T(8,128)}, u32[]{:S(2)}) copy-start(f32[16,128]{1,0:T(8,128)} %param.8) | copy-start | bytes 24580
  282.6 18.4 %copy-start.4 = (f32[16,128]{1,0:T(8,128)S(1)}, f32[16,128]{1,0:T(8,128)}, u32[]{:S(2)}) copy-start(f32[16,128]{1,0:T(8,128)} %param.9) | copy-start | bytes 24580
